TPU v7x, 64 devices: a 2x2x8 block of a 4x4x8 slice. The times are simulated.
64 devices in a mesh: rep: 4 (over x, y), dp: 16 (over z, core).
Axes of the slice: x: 2, y: 2, z: 8, core: 2. Of those that a mesh axis runs over, the one named last changes fastest.
The devices are a block of a 4x4x8 slice.
Arguments:
- a: bfloat16 [64, 4, 4096, 896], P(('rep', 'dp')), parts along dimension 0
- g: bfloat16 [64, 4, 4096, 2560], P(('rep', 'dp')), parts along dimension 0
Outputs:
- output: bfloat16 [16, 896, 2560], P('rep'), parts along dimension 0
There are 4 independent parts. A program takes and returns all parts, laid end to end along the dimension named above; each array names one.
All inputs are finite; a program needn't handle non-finite values.
Results may differ from a plain program's by a relative error of at most 0.012.
Values are sent between devices in bfloat16 or wider.
A program may use at most 768 MiB of HBM per device.

v0:
```python
import jax
import jax.numpy as jnp


def solution(mesh):
    groups = mesh.shape["rep"]

    def step(a, g):
        a, g = (t.reshape(groups, -1, *t.shape[1:]) for t in (a, g))
        sums = jnp.einsum("rsntd,rsntf->rndf", a, g, preferred_element_type=jnp.float32)
        return sums.astype(jnp.bfloat16).reshape(-1, *sums.shape[2:])

    return step
```

profile of v0, /device:TPU:21, one launch (start us, length us, event | category | flops | bytes accessed | tf_op | source)
XLA Modules:
  0.0 493.5 jit_solution(5207049383093108906)
XLA Ops:
  0.0 87.4 %fusion.3 = f32[1,4,896,2560]{3,2,1,0:T(8,128)} fusion(bf16[1,4,4096,2560]{3,2,1,0:T(8,128)(2,1)} %param.1, bf16[1,4,4096,896]{3,2,1,0:T(8,128)(2,1)} %param), kind=kOutput, calls=%fused_computation.3 | convolution fusion | flops 75161927680 | bytes 149946368 | tf_op jit(solution)/rsntd,rsntf->rndf/dot_general | solution.py:10
  87.4 406.1 %all-reduce.2 = bf16[1,4,896,2560]{3,2,1,0:T(8,128)(2,1)} all-reduce(f32[1,4,896,2560]{3,2,1,0:T(8,128)} %fusion.3), channel_id=1, replica_groups=[4,16]<=[64], use_global_device_ids=true, to_apply=%add.clone | all-reduce | flops 9175040 | bytes 55050240 | tf_op jit(solution)/rsntd,rsntf->rndf/dot_general | solution.py:10
where the time goes:
time: 494 us; the launch traced here: 493 us
  blocking collectives  406 us (82%)
  matrix products  87.4 us (18%)
    dot_general x1, blocking collectives, step(): jnp.einsum('rsntd,rsntf->rndf', a, g, preferred_element_type=jnp.float32)  406 us
    dot_general x1, matrix products, step(): jnp.einsum('rsntd,rsntf->rndf', a, g, preferred_element_type=jnp.float32)  87.4 us

commit v1 on v0

v1 whole, which is shorter than its diff:
```python
import functools

import jax
import jax.numpy as jnp
from jax import lax
from jax.experimental import pallas as pl
from jax.experimental.pallas import tpu as pltpu
from jax.sharding import PartitionSpec as P

MESH = pl.DeviceIdType.MESH
CORES = 2
NB = 256
AB = 128
GSLOTS = 4
ROWS = 512


def kernel(devices, a_ref, g_ref, out_ref, at, gbuf, abuf, acc, stage, sums, gsem, asem, stage_sem, sums_sem,
           ring_send, ring_recv, pair_send, pair_recv, done_sem):
    me = lax.axis_index("dp")
    chips = devices // CORES
    z, core = lax.div(me, CORES), lax.rem(me, CORES)
    peer = me + 1 - 2 * core
    onward = (lax.rem(me + CORES, devices), lax.rem(me + devices - CORES, devices))
    _, matrices, depth, d_out = a_ref.shape
    ff = g_ref.shape[3]
    half, mine = d_out // 2, d_out // 4
    per_matrix = chips // matrices
    tiles = ff // per_matrix // NB
    steps = chips * tiles
    KB = min(2048, depth)
    early = tiles // 2
    late = tiles - early
    turn = chips * early

    def chunk(d, s):
        c = lax.rem(z + jnp.where(d == 0, chips - 1 - s, 1 + s), chips)
        return lax.div(c, per_matrix), lax.rem(c, per_matrix)

    def place(d, s, t):
        n, side = chunk(d, s)
        return n, pl.ds(pl.multiple_of((side * tiles + t) * NB, NB), NB)

    own = [pl.ds(pl.multiple_of(d * half + core * mine, 16), mine) for d in range(2)]
    theirs = [pl.ds(pl.multiple_of(d * half + (1 - core) * mine, 16), mine) for d in range(2)]
    own_acc = pl.ds(pl.multiple_of(core * mine, 16), mine)
    their_acc = pl.ds(pl.multiple_of((1 - core) * mine, 16), mine)

    def split(k):
        first = k < turn
        width = jnp.where(first, early, late)
        r = jnp.where(first, k, k - turn)
        return lax.div(r, width), lax.rem(r, width) + jnp.where(first, 0, early)

    def g_load(k, d):
        s, t = split(k)
        n, cols = place(d, s, t)
        slot = d + 2 * lax.rem(k, 2)
        return pltpu.make_async_copy(g_ref.at[0, n, :, cols], gbuf.at[slot], gsem.at[slot])

    def a_load(d, s):
        n, _ = chunk(d, s)
        lo = pl.multiple_of(d * (d_out - ROWS), AB)
        return pltpu.make_async_copy(a_ref.at[0, n, :, pl.ds(lo, ROWS)], abuf, asem)

    def fresh(s):
        return lax.rem(z + s, per_matrix)

    def transpose(d, s):
        n, _ = chunk(d, s)
        lo = d * (d_out - ROWS)

        def block(i, _):
            k, j = lax.div(i, ROWS // AB), lax.rem(i, ROWS // AB)
            ks = pl.ds(pl.multiple_of(k * KB, KB), KB)
            x = abuf[ks, pl.ds(pl.multiple_of(j * AB, AB), AB)]
            at[n, pl.ds(pl.multiple_of(lo + j * AB, AB), AB), ks] = x.T
            return 0

        lax.fori_loop(0, depth // KB * (ROWS // AB), block, 0)

    def ring_sum(d, s, n, cols, t):
        return pltpu.make_async_remote_copy(
            src_ref=sums.at[d, t], dst_ref=out_ref.at[n, own[d], cols], send_sem=sums_sem.at[d, t],
            recv_sem=ring_recv.at[d, s + 1, t], device_id={"dp": onward[d]}, device_id_type=MESH)

    def ring(d, src_idx, n, cols, dst_idx, t):
        piece = out_ref.at[n, own[d], cols]
        return pltpu.make_async_remote_copy(
            src_ref=piece, dst_ref=piece, send_sem=ring_send.at[d, src_idx, t], recv_sem=ring_recv.at[d, dst_idx, t],
            device_id={"dp": onward[d]}, device_id_type=MESH)

    def pair_out(d, k):
        s, t = split(k)
        n, cols = place(d, s, t)
        slot = lax.rem(k, 2)
        return pltpu.make_async_remote_copy(
            src_ref=stage.at[d, slot], dst_ref=out_ref.at[n, own[d], cols], send_sem=stage_sem.at[d, slot],
            recv_sem=pair_recv.at[d, s, t], device_id={"dp": peer}, device_id_type=MESH)

    def pair_share(d, j, n, cols, t):
        piece = out_ref.at[n, own[d], cols]
        return pltpu.make_async_remote_copy(
            src_ref=piece, dst_ref=piece, send_sem=pair_send.at[d, j, t], recv_sem=pair_recv.at[d, j, t],
            device_id={"dp": peer}, device_id_type=MESH)

    def products(k):
        s, _ = split(k)

        @pl.when(k + 1 < steps)
        def _():
            for d in range(2):
                g_load(k + 1, d).start()

        for d in range(2):
            g_load(k, d).wait()
        slot = lax.rem(k, 2)
        for d in range(2):
            n, _ = chunk(d, s)
            acc[slot, d] = jnp.dot(
                at[n, pl.ds(d * half, half), :], gbuf[d + 2 * slot], preferred_element_type=jnp.float32)

    def pair_up(k):
        slot = lax.rem(k, 2)

        @pl.when(k >= 2)
        def _():
            for d in range(2):
                pair_out(d, k - 2).wait_send()

        for d in range(2):
            stage[d, slot] = acc[slot, d, their_acc, :].astype(stage.dtype)
        for d in range(2):
            pair_out(d, k).start()

    def add(k, d):
        s, t = split(k)
        n, cols = place(d, s, t)

        @pl.when(s > 0)
        def _():
            ring_sum(d, s - 1, n, cols, t).wait()

        pair_share(d, s, n, cols, t).wait_recv()
        total = acc[lax.rem(k, 2), d, own_acc, :] + out_ref[n, theirs[d], cols].astype(jnp.float32)
        before = out_ref[n, own[d], cols].astype(jnp.float32)
        total = jnp.where(s > 0, total + before, total).astype(out_ref.dtype)

        @pl.when(s < chips - 1)
        def _():
            sums[d, t] = total
            ring_sum(d, s, n, cols, t).start()

        @pl.when(s == chips - 1)
        def _():
            out_ref[n, own[d], cols] = total
            ring(d, s, n, cols, 0, t).start()

    def greet():
        pl.semaphore_signal(done_sem, inc=1, device_id={"dp": peer}, device_id_type=MESH)

    def share_own(lo, hi):
        pl.semaphore_wait(done_sem, 1)

        def one(t, _):
            for d in range(2):
                n, cols = place(d, chips - 1, t)
                pair_share(d, chips - 1, n, cols, t).start()
            return 0

        lax.fori_loop(lo, hi, one, 0)

    def gather(j, t):
        for d in range(2):
            n, cols = place(d, j, t)
            ring(d, j, n, cols, j, t).wait_recv()

            @pl.when(j < chips - 2)
            def _():
                ring(d, j, n, cols, j + 1, t).start()

            pair_share(d, j, n, cols, t).start()

    barrier = pltpu.get_barrier_semaphore()
    for other in (*onward, peer):
        pl.semaphore_signal(barrier, inc=1, device_id={"dp": other}, device_id_type=MESH)
    for d in range(2):
        a_load(d, 0).start()
        if d == 0:
            for e in range(2):
                g_load(0, e).start()
        a_load(d, 0).wait()
        transpose(d, 0)
    a_load(fresh(1), 1).start()
    pl.semaphore_wait(barrier, 3)

    def reduce_early(k, _):
        s, t = split(k)
        products(k)
        pair_up(k)

        @pl.when(k > 0)
        def _():
            for d in range(2):
                add(k - 1, d)

        @pl.when(jnp.logical_and(t == 0, s + 1 < chips - 1))
        def _():
            a_load(fresh(s + 1), s + 1).wait()
            transpose(fresh(s + 1), s + 1)

            @pl.when(s + 2 < chips - 1)
            def _():
                a_load(fresh(s + 2), s + 2).start()

        return 0

    lax.fori_loop(0, turn, reduce_early, 0)

    hops, span = (chips - 1) * early, chips * late - 2

    def reduce_late(i, _):
        k = turn + i
        products(k)
        pair_up(k)
        for d in range(2):
            add(k - 1, d)

        @pl.when(i == 0)
        def _():
            greet()

        @pl.when(i == 1)
        def _():
            share_own(0, early)

        q = lax.div((i - 2) * hops, span)

        @pl.when(jnp.logical_and(i >= 2, lax.div((i - 1) * hops, span) > q))
        def _():
            gather(lax.div(q, early), lax.rem(q, early))

        return 0

    lax.fori_loop(0, chips * late, reduce_late, 0)
    for d in range(2):
        add(steps - 1, d)
    greet()
    share_own(early, tiles)

    def gather_late(i, _):
        gather(lax.div(i, late), early + lax.rem(i, late))
        return 0

    lax.fori_loop(0, (chips - 1) * late, gather_late, 0)

    def drain(i, _):
        j, t = lax.div(i, tiles), lax.rem(i, tiles)
        for d in range(2):
            n, cols = place(d, j, t)
            last = pair_share(d, j, n, cols, t)
            last.wait_send()
            last.wait_recv()

            @pl.when(j != chips - 2)
            def _():
                ring(d, j, n, cols, 0, t).wait_send()
        return 0

    lax.fori_loop(0, steps, drain, 0)
    for d in range(2):
        for k in (steps - 2, steps - 1):
            pair_out(d, k).wait_send()


def solution(mesh):
    devices = mesh.shape["dp"]

    def step(a, g):
        _, matrices, depth, d_out = a.shape
        ff = g.shape[3]
        chips = devices // CORES
        tiles = ff // (chips // matrices) // NB
        per = (2, chips, tiles)
        return pl.pallas_call(
            functools.partial(kernel, devices),
            out_shape=pltpu.VMEM((matrices, d_out, ff), a.dtype),
            in_specs=[pl.BlockSpec(memory_space=pl.ANY)] * 2,
            out_specs=pl.BlockSpec(memory_space=pltpu.VMEM),
            scratch_shapes=[
                pltpu.VMEM((matrices, d_out, depth), a.dtype),
                pltpu.VMEM((GSLOTS, depth, NB), g.dtype),
                pltpu.VMEM((depth, ROWS), a.dtype),
                pltpu.VMEM((2, 2, d_out // 2, NB), jnp.float32),
                pltpu.VMEM((2, 2, d_out // 4, NB), a.dtype),
                pltpu.VMEM((2, tiles, d_out // 4, NB), a.dtype),
                pltpu.SemaphoreType.DMA((GSLOTS,)),
                pltpu.SemaphoreType.DMA,
                pltpu.SemaphoreType.DMA((2, 2)),
                pltpu.SemaphoreType.DMA((2, tiles)),
                pltpu.SemaphoreType.DMA(per),
                pltpu.SemaphoreType.DMA(per),
                pltpu.SemaphoreType.DMA(per),
                pltpu.SemaphoreType.DMA(per),
                pltpu.SemaphoreType.REGULAR,
            ],
            compiler_params=pltpu.CompilerParams(
                collective_id=0, has_side_effects=True, vmem_limit_bytes=45 * 2**20,
            ),
        )(a, g)

    return jax.shard_map(
        step,
        mesh=mesh,
        in_specs=(P(("rep", "dp")), P(("rep", "dp"))),
        out_specs=P("rep"),
        check_vma=False,
    )
```

time: 494 us -> 219 us (0.44)
  blocking collectives: 406 us -> 0 us
  Pallas kernels: 0 us -> 212 us
  matrix products: 87.4 us -> 0 us
  local copies, waits for them, and re-layouts: 0 us -> 6.68 us
    dot_general x1 -> x0, blocking collectives: 406 us -> none  [step(): jnp.einsum('rsntd,rsntf->rndf', a, g, preferred_element_type=jnp.float32)]
    pallas_call x0 -> x1, Pallas kernels: none -> 212 us  [step(): pl.pallas_call(functools.partial(kernel, devices), out_shape=pltpu.VMEM((...]
    dot_general x1 -> x0, matrix products: 87.4 us -> none  [step(): jnp.einsum('rsntd,rsntf->rndf', a, g, preferred_element_type=jnp.float32)]
    unnamed x0 -> x1, local copies, waits for them, and re-layouts: none -> 6.68 us
where the time goes in v1:
time: 219 us
  Pallas kernels  212 us (97%)
  local copies, waits for them, and re-layouts  6.68 us (3%)
    pallas_call x1, Pallas kernels, step(): pl.pallas_call(functools.partial(kernel, devices), out_shape=pltpu.VMEM((...  212 us
    unnamed x1, local copies, waits for them, and re-layouts  6.68 us

profile of v1, /device:TPU:21, one launch (start us, length us, event | category | flops | bytes accessed | tf_op | source)
XLA Modules:
  0.0 218.7 jit_solution(10068144623279336430)
XLA Ops:
  0.0 212.0 %shard_map.28 = bf16[4,896,2560]{2,1,0:T(8,128)(2,1)S(1)} custom-call(bf16[1,4,4096,896]{3,2,1,0:T(8,128)(2,1)} %a_ref.1, bf16[1,4,4096,2560]{3,2,1,0:T(8,128)(2,1)} %g_ref.1), custom_call_target="tpu_custom_call" | custom-call | tf_op jit(solution)/shard_map/pallas_call | solution.py:285
  212.1 6.7 %copy.4 = bf16[4,896,2560]{2,1,0:T(8,128)(2,1)} copy(bf16[4,896,2560]{2,1,0:T(8,128)(2,1)S(1)} %shard_map.28) | data formatting | bytes 36700160

commit v2 on v0

v2 whole, which is shorter than its diff:
```python
import functools

import jax
import jax.numpy as jnp
from jax import lax
from jax.experimental import pallas as pl
from jax.experimental.pallas import tpu as pltpu
from jax.sharding import PartitionSpec as P

MESH = pl.DeviceIdType.MESH
CORES = 2
NB = 256
AB = 128
GDEPTH = 3
PIECES = 4
ROWS = 512
SLOTS = 3
LAG = 1


def kernel(devices, a_ref, g_ref, out_ref, at, gbuf, abuf, acc, stage, sums, gsem, asem, stage_sem, sums_sem,
           ring_send, ring_recv, pair_send, pair_recv, done_sem):
    me = lax.axis_index("dp")
    chips = devices // CORES
    z, core = lax.div(me, CORES), lax.rem(me, CORES)
    peer = me + 1 - 2 * core
    ahead = lax.rem(me + jnp.where(core == 0, CORES, devices - CORES), devices)
    behind = lax.rem(me + jnp.where(core == 0, devices - CORES, CORES), devices)
    _, matrices, depth, d_out = a_ref.shape
    ff = g_ref.shape[3]
    half = d_out // 2
    per_matrix = chips // matrices
    tiles = ff // per_matrix // NB
    steps = chips * tiles
    KB = depth // PIECES

    def chunk(d, s):
        c = lax.rem(z + jnp.where(d == 0, chips - 1 - s, 1 + s), chips)
        return lax.div(c, per_matrix), lax.rem(c, per_matrix)

    def place(d, s, t):
        n, side = chunk(d, s)
        return n, pl.ds(pl.multiple_of((side * tiles + t) * NB, NB), NB)

    own = pl.ds(pl.multiple_of(core * half, 16), half)
    theirs = pl.ds(pl.multiple_of((1 - core) * half, 16), half)

    def split(k):
        return lax.div(k, tiles), lax.rem(k, tiles)

    def g_load(k, d):
        s, t = split(k)
        n, cols = place(d, s, t)
        slot = d + 2 * lax.rem(k, GDEPTH)
        return pltpu.make_async_copy(g_ref.at[0, n, :, cols], gbuf.at[slot], gsem.at[slot])

    def a_load(d, s, q):
        n, _ = chunk(d, s)
        lo = pl.multiple_of(d * (d_out - ROWS), AB)
        return pltpu.make_async_copy(
            a_ref.at[0, n, pl.ds(pl.multiple_of(q * KB, KB), KB), pl.ds(lo, ROWS)],
            abuf.at[lax.rem(q, 2)], asem.at[lax.rem(q, 2)])

    def fresh(s):
        return lax.rem(z + s, per_matrix)

    def transpose(d, s, q):
        n, _ = chunk(d, s)
        lo = d * (d_out - ROWS)

        at[n, pl.ds(pl.multiple_of(lo, AB), ROWS), pl.ds(pl.multiple_of(q * KB, KB), KB)] = abuf[lax.rem(q, 2)].T

    def ring_sum(s, n, cols, t):
        slot = lax.rem(s * tiles + t, SLOTS)
        return pltpu.make_async_remote_copy(
            src_ref=sums.at[slot], dst_ref=out_ref.at[n, own, cols], send_sem=sums_sem.at[slot],
            recv_sem=ring_recv.at[s + 1, t], device_id={"dp": ahead}, device_id_type=MESH)

    def ring(src_idx, n, cols, dst_idx, t):
        piece = out_ref.at[n, own, cols]
        return pltpu.make_async_remote_copy(
            src_ref=piece, dst_ref=piece, send_sem=ring_send.at[src_idx, t], recv_sem=ring_recv.at[dst_idx, t],
            device_id={"dp": ahead}, device_id_type=MESH)

    def pair_out(k):
        s, t = split(k)
        n, cols = place(1 - core, s, t)
        slot = lax.rem(k, 2)
        return pltpu.make_async_remote_copy(
            src_ref=stage.at[slot], dst_ref=out_ref.at[n, own, cols], send_sem=stage_sem.at[slot],
            recv_sem=pair_recv.at[s, t], device_id={"dp": peer}, device_id_type=MESH)

    def pair_share(j, n, cols, t):
        piece = out_ref.at[n, own, cols]
        return pltpu.make_async_remote_copy(
            src_ref=piece, dst_ref=piece, send_sem=pair_send.at[j, t], recv_sem=pair_recv.at[j, t],
            device_id={"dp": peer}, device_id_type=MESH)

    def fetch(k):
        @pl.when(k + GDEPTH - 1 < steps)
        def _():
            for d in range(2):
                g_load(k + GDEPTH - 1, d).start()

        for d in range(2):
            g_load(k, d).wait()

    def free_stage(k):
        @pl.when(k >= 2)
        def _():
            pair_out(k - 2).wait_send()

    def products(k, beside=lambda: None):
        s, _ = split(k)
        terms = []
        for d in range(2):
            n, _ = chunk(d, s)
            terms.append(jnp.dot(
                at[n, pl.ds(d * half, half), :], gbuf[d + 2 * lax.rem(k, GDEPTH)], preferred_element_type=jnp.float32))
        beside()
        acc[lax.rem(k, LAG + 1)] = jnp.where(core == 0, terms[0], terms[1])
        stage[lax.rem(k, 2)] = jnp.where(core == 0, terms[1], terms[0]).astype(stage.dtype)

    def await_terms(k):
        s, t = split(k)
        n, cols = place(core, s, t)

        @pl.when(s > 0)
        def _():
            ring_sum(s - 1, n, cols, t).wait_recv()

        pair_share(s, n, cols, t).wait_recv()

        @pl.when(jnp.logical_and(k >= SLOTS, k - SLOTS < steps - tiles))
        def _():
            s0, t0 = split(k - SLOTS)
            n0, cols0 = place(core, s0, t0)
            ring_sum(s0, n0, cols0, t0).wait_send()

    def add(k):
        s, t = split(k)
        n, cols = place(core, s, t)
        total = acc[lax.rem(k, LAG + 1)] + out_ref[n, theirs, cols].astype(jnp.float32)
        before = out_ref[n, own, cols].astype(jnp.float32)
        sums[lax.rem(k, SLOTS)] = jnp.where(s > 0, total + before, total).astype(sums.dtype)

    def send(k):
        s, t = split(k)
        n, cols = place(core, s, t)

        @pl.when(s < chips - 1)
        def _():
            ring_sum(s, n, cols, t).start()

        @pl.when(s == chips - 1)
        def _():
            out_ref[n, own, cols] = sums[lax.rem(k, SLOTS)]
            ring(s, n, cols, 0, t).start()

    barrier = pltpu.get_barrier_semaphore()
    for other in (ahead, behind, peer):
        pl.semaphore_signal(barrier, inc=1, device_id={"dp": other}, device_id_type=MESH)
    def first_load(d, e):
        n, _ = chunk(d, 0)
        return pltpu.make_async_copy(
            a_ref.at[0, n, :, pl.ds(d * (d_out - ROWS) + e * NB, NB)], gbuf.at[2 + 2 * d + e], gsem.at[2 + 2 * d + e])

    for d in range(2):
        for e in range(2):
            first_load(d, e).start()
    for d in range(2):
        g_load(0, d).start()
    for q in range(2):
        a_load(fresh(1), 1, q).start()
    for d in range(2):
        n, _ = chunk(d, 0)
        for e in range(2):
            first_load(d, e).wait()

            def turn(q, _):
                ks = pl.ds(pl.multiple_of(q * KB, KB), KB)
                at[n, pl.ds(d * (d_out - ROWS) + e * NB, NB), ks] = gbuf[2 + 2 * d + e, ks, :].T
                return 0

            lax.fori_loop(0, PIECES, turn, 0)
    for k in range(1, GDEPTH - 1):
        for d in range(2):
            g_load(k, d).start()
    pl.semaphore_wait(barrier, 3)

    def next_matrix(k):
        s, q = split(k)

        @pl.when(jnp.logical_and(q < PIECES, s + 1 < chips - 1))
        def _():
            a_load(fresh(s + 1), s + 1, q).wait()
            transpose(fresh(s + 1), s + 1, q)

            @pl.when(q < PIECES - 2)
            def _():
                a_load(fresh(s + 1), s + 1, q + 2).start()

            @pl.when(jnp.logical_and(q >= PIECES - 2, s + 2 < chips - 1))
            def _():
                a_load(fresh(s + 2), s + 2, q + 2 - PIECES).start()

    def reduce_step(k, _):
        fetch(k)
        free_stage(k)
        products(k)
        pair_out(k).start()

        @pl.when(k >= LAG)
        def _():
            await_terms(k - LAG)
            add(k - LAG)
            send(k - LAG)

        next_matrix(k)
        return 0

    lax.fori_loop(0, steps, reduce_step, 0)

    def last_steps(k, _):
        await_terms(k)
        add(k)
        send(k)
        return 0

    lax.fori_loop(steps - LAG, steps, last_steps, 0)

    pl.semaphore_signal(done_sem, inc=1, device_id={"dp": peer}, device_id_type=MESH)
    pl.semaphore_wait(done_sem, 1)

    def share_own(t, _):
        n, cols = place(core, chips - 1, t)
        pair_share(chips - 1, n, cols, t).start()
        return 0

    lax.fori_loop(0, tiles, share_own, 0)

    def gather(i, _):
        j, t = split(i)
        n, cols = place(core, j, t)
        ring(j, n, cols, j, t).wait_recv()

        @pl.when(j < chips - 2)
        def _():
            ring(j, n, cols, j + 1, t).start()

        pair_share(j, n, cols, t).start()
        return 0

    lax.fori_loop(0, (chips - 1) * tiles, gather, 0)

    def drain(i, _):
        j, t = split(i)
        n, cols = place(core, j, t)
        last = pair_share(j, n, cols, t)
        last.wait_send()
        last.wait_recv()

        @pl.when(j != chips - 2)
        def _():
            ring(j, n, cols, 0, t).wait_send()
        return 0

    lax.fori_loop(0, steps, drain, 0)
    for k in (steps - 2, steps - 1):
        pair_out(k).wait_send()


def solution(mesh):
    devices = mesh.shape["dp"]

    def step(a, g):
        _, matrices, depth, d_out = a.shape
        ff = g.shape[3]
        chips = devices // CORES
        tiles = ff // (chips // matrices) // NB
        per = (chips, tiles)
        return pl.pallas_call(
            functools.partial(kernel, devices),
            out_shape=pltpu.VMEM((matrices, d_out, ff), a.dtype),
            in_specs=[pl.BlockSpec(memory_space=pl.ANY)] * 2,
            out_specs=pl.BlockSpec(memory_space=pltpu.VMEM),
            scratch_shapes=[
                pltpu.VMEM((matrices, d_out, depth), a.dtype),
                pltpu.VMEM((2 * GDEPTH, depth, NB), g.dtype),
                pltpu.VMEM((2, depth // PIECES, ROWS), a.dtype),
                pltpu.VMEM((LAG + 1, d_out // 2, NB), jnp.float32),
                pltpu.VMEM((2, d_out // 2, NB), a.dtype),
                pltpu.VMEM((SLOTS, d_out // 2, NB), a.dtype),
                pltpu.SemaphoreType.DMA((2 * GDEPTH,)),
                pltpu.SemaphoreType.DMA((2,)),
                pltpu.SemaphoreType.DMA((2,)),
                pltpu.SemaphoreType.DMA((SLOTS,)),
                pltpu.SemaphoreType.DMA(per),
                pltpu.SemaphoreType.DMA(per),
                pltpu.SemaphoreType.DMA(per),
                pltpu.SemaphoreType.DMA(per),
                pltpu.SemaphoreType.REGULAR,
            ],
            compiler_params=pltpu.CompilerParams(
                collective_id=0, has_side_effects=True, vmem_limit_bytes=48_600_000,
            ),
        )(a, g)

    return jax.shard_map(
        step,
        mesh=mesh,
        in_specs=(P(("rep", "dp")), P(("rep", "dp"))),
        out_specs=P("rep"),
        check_vma=False,
    )
```

time: 494 us -> 205 us (0.41)
  blocking collectives: 406 us -> 0 us
  Pallas kernels: 0 us -> 198 us
  matrix products: 87.4 us -> 0 us
  local copies, waits for them, and re-layouts: 0 us -> 6.68 us
    dot_general x1 -> x0, blocking collectives: 406 us -> none  [step(): jnp.einsum('rsntd,rsntf->rndf', a, g, preferred_element_type=jnp.float32)]
    pallas_call x0 -> x1, Pallas kernels: none -> 198 us  [step(): pl.pallas_call(functools.partial(kernel, devices), out_shape=pltpu.VMEM((...]
    dot_general x1 -> x0, matrix products: 87.4 us -> none  [step(): jnp.einsum('rsntd,rsntf->rndf', a, g, preferred_element_type=jnp.float32)]
    unnamed x0 -> x1, local copies, waits for them, and re-layouts: none -> 6.68 us
where the time goes in v2:
time: 205 us
  Pallas kernels  198 us (97%)
  local copies, waits for them, and re-layouts  6.68 us (3%)
    pallas_call x1, Pallas kernels, step(): pl.pallas_call(functools.partial(kernel, devices), out_shape=pltpu.VMEM((...  198 us
    unnamed x1, local copies, waits for them, and re-layouts  6.68 us

profile of v2, /device:TPU:21, one launch (start us, length us, event | category | flops | bytes accessed | tf_op | source)
XLA Modules:
  0.0 204.6 jit_solution(495688571688850415)
XLA Ops:
  0.0 197.9 %shard_map.28 = bf16[4,896,2560]{2,1,0:T(8,128)(2,1)S(1)} custom-call(bf16[1,4,4096,896]{3,2,1,0:T(8,128)(2,1)} %a_ref.1, bf16[1,4,4096,2560]{3,2,1,0:T(8,128)(2,1)} %g_ref.1), custom_call_target="tpu_custom_call" | custom-call | tf_op jit(solution)/shard_map/pallas_call | solution.py:282
  197.9 6.7 %copy.4 = bf16[4,896,2560]{2,1,0:T(8,128)(2,1)} copy(bf16[4,896,2560]{2,1,0:T(8,128)(2,1)S(1)} %shard_map.28) | data formatting | bytes 36700160
